TPU v7x, 128 devices: a whole 4x4x4 slice. The times are simulated.
128 devices in a mesh: mem: 4 (over x_lo, core), slab: 32 (over z, y, x_hi).
Axes of the slice: x: 4 (x_hi: 2, x_lo: 2; x = x_hi * 2 + x_lo), y: 4, z: 4, core: 2. Of those that a mesh axis runs over, the one named last changes fastest.
Arguments:
- anomalies: bfloat16 [8, 4096, 4096], P('mem', 'slab'), may hold values from -2.390625 to 2.390625
- increment: float32 [4096, 4096], P('slab'), may hold values from -6 to 6
- spectrum: float32 [4096, 4096], P(None, 'slab'), may hold values from 0.01 to 2, as said below
Outputs:
- product: float32 [4096, 4096], P('slab')
Inputs may be any that keep to these rules, and one draw needn't show every extreme that they name: spectrum[k, l] equals spectrum[(4096 - k) % 4096, (4096 - l) % 4096], and is positive.
All inputs are finite; a program needn't handle non-finite values.
Results may differ from a plain program's by a relative error of at most 0.0003.
Values sent between devices are 32-bit elements; how exact they have to be, the bound alone decides.
A program may use at most 128 MiB of HBM per device.

v0:
```python
import math

import jax
import jax.numpy as jnp
import numpy as np
from jax import lax
from jax.experimental import pallas as pl
from jax.experimental.pallas import tpu as pltpu
from jax.sharding import PartitionSpec as P

MESH = pl.DeviceIdType.MESH
F32 = jnp.float32
BF16 = jnp.bfloat16
ROOT_HALF = math.sqrt(0.5)

ROUNDS = (
    (2, 2), (1, 1), (3, 3), (0, 0), (1, 3), (3, 1), (0, 2), (2, 0),
    (1, 0), (3, 2), (1, 2), (3, 0), (0, 1), (2, 3), (2, 1), (0, 3),
)
OFFSETS = tuple(
    offset
    for a, b in ROUNDS
    for offset in ((a, b, 1), ((a + 2) % 4, (b + 2) % 4, 0))
    if offset != (0, 0, 0)
)


def constant_tables():
    index = np.arange(128)
    angle = 2.0 * np.pi / 128 * (np.outer(index, index) % 128)
    cos, sin = np.cos(angle), np.sin(angle)
    tables = []
    for sign in (-1.0, 1.0):
        block = np.block([[cos, sign * sin], [-sign * sin, cos]])
        if sign < 0:
            flipped = block.T
            high = flipped.astype(BF16)
            low = (flipped - high.astype(np.float64)).astype(BF16)
            tables.append(np.concatenate([high, high, low], axis=1))
        high = block.astype(BF16)
        low = (block - high.astype(np.float64)).astype(BF16)
        tables.append(np.concatenate([high, high, low], axis=0))
    twist = 2.0 * np.pi / 4096 * np.outer(np.arange(32), index)
    twist = np.stack([np.cos(twist), np.sin(twist)]).astype(np.float32)
    twist = np.broadcast_to(twist[:, :, None, :], (2, 32, 8, 128)).copy()
    return tables, twist


def short_transform(values, sign):
    count = len(values)
    if count == 1:
        return values
    even = short_transform(values[0::2], sign)
    odd = short_transform(values[1::2], sign)
    first, second = [], []
    for k in range(count // 2):
        (er, ei), (xr, xi) = even[k], odd[k]
        if k == 0:
            tr, ti = xr, xi
        elif 4 * k == count:
            if sign > 0:
                first.append((er - xi, ei + xr))
                second.append((er + xi, ei - xr))
            else:
                first.append((er + xi, ei - xr))
                second.append((er - xi, ei + xr))
            continue
        elif 8 * k == count:
            tr = (xr - sign * xi if sign > 0 else xr + xi) * ROOT_HALF
            ti = (xi + xr if sign > 0 else xi - xr) * ROOT_HALF
        elif 8 * k == 3 * count:
            tr = (xr + xi if sign > 0 else xr - xi) * -ROOT_HALF
            ti = (xr - xi if sign > 0 else -xr - xi) * ROOT_HALF
        else:
            cos = math.cos(2.0 * math.pi * k / count)
            sin = sign * math.sin(2.0 * math.pi * k / count)
            tr = xr * cos - xi * sin
            ti = xr * sin + xi * cos
        first.append((er + tr, ei + ti))
        second.append((er - tr, ei - ti))
    return first + second


def three_parts(x):
    high = x.astype(BF16)
    low = (x - high.astype(F32)).astype(BF16)
    return jnp.concatenate([high, low, high], axis=1)


def kernel(
    anomalies, increment, spectrum, forward_flip, forward, inverse, twist, out,
    anom, incr, spec, spec_flip, field_re, field_im, work, send_a, recv_a,
    column, send_b, recv_b, part, recv_part, pair, recv_pair, total,
    load_sem, send_a_sem, recv_a_sem, send_b_sem, recv_b_sem, part_sems, pair_sems, total_sems,
    out_sem,
):
    me = lax.axis_index("slab")
    mem = lax.axis_index("mem")
    z, y, x = me // 8, (me // 2) % 4, me % 2
    core = mem % 2
    other_core = (mem // 2) * 2 + (1 - core)
    other_chip = (1 - mem // 2) * 2 + core

    def slab_at(offset):
        dz, dy, dx = offset
        return ((z + dz) % 4) * 8 + ((y + dy) % 4) * 2 + (x + dx) % 2

    loads = [
        pltpu.make_async_copy(anomalies, anom, load_sem.at[0]),
        pltpu.make_async_copy(increment, incr, load_sem.at[1]),
        pltpu.make_async_copy(spectrum, spec, load_sem.at[2]),
    ]
    for copy in loads:
        copy.start()

    barrier = pltpu.get_barrier_semaphore()
    for offset in OFFSETS:
        pl.semaphore_signal(
            barrier, inc=1, device_id={"mem": mem, "slab": slab_at(offset)}, device_id_type=MESH
        )
    for mate in (other_core, other_chip):
        pl.semaphore_signal(
            barrier, inc=1, device_id={"mem": mate, "slab": me}, device_id_type=MESH
        )

    sub = lax.broadcasted_iota(jnp.int32, (16, 8, 128), 1)
    lower = sub < 4

    def interlaced(a, b):
        even = jnp.where(lower, a, pltpu.roll(b, 4, 1))
        odd = jnp.where(lower, pltpu.roll(a, 4, 1), b)
        return even, odd

    def twisted(values, sign):
        result = [values[0]]
        for k in range(1, 32):
            re, im = values[k]
            cos, sin = twist[0, k], twist[1, k]
            if sign > 0:
                result.append((re * cos - im * sin, re * sin + im * cos))
            else:
                result.append((re * cos + im * sin, im * cos - re * sin))
        return result

    loads[0].wait()
    loads[1].wait()

    def multiply(b, carry):
        rows = pl.ds(pl.multiple_of(b * 16, 16), 16)
        step = incr[rows, :]
        field_re[rows, :] = anom[0, rows, :].astype(F32) * step
        field_im[rows, :] = anom[1, rows, :].astype(F32) * step
        return carry

    lax.fori_loop(0, 8, multiply, 0)

    def forward_rows(g, carry):
        rows = pl.ds(pl.multiple_of(g * 8, 8), 8)
        values = [
            (field_re[rows, 128 * a : 128 * a + 128], field_im[rows, 128 * a : 128 * a + 128])
            for a in range(32)
        ]
        values = twisted(short_transform(values, -1), -1)
        for a in range(32):
            work[a, rows, 0:128] = values[a][0]
            work[a, rows, 128:256] = values[a][1]
        return carry

    lax.fori_loop(0, 16, forward_rows, 0)

    pl.semaphore_wait(barrier, len(OFFSETS) + 2)

    def send_copy(source, target, send_sem, recv_sem, chunk, slab):
        return pltpu.make_async_remote_copy(
            src_ref=source.at[chunk, slab],
            dst_ref=target.at[chunk, me],
            send_sem=send_sem.at[chunk],
            recv_sem=recv_sem.at[chunk],
            device_id={"mem": mem, "slab": slab},
            device_id_type=MESH,
        )

    def whole_copy(source, target, send_sem, recv_sem, chunk):
        return pltpu.make_async_remote_copy(
            src_ref=source.at[chunk, 0:31],
            dst_ref=target.at[chunk, 0:31],
            send_sem=send_sem.at[chunk],
            recv_sem=recv_sem.at[chunk],
            device_id={"mem": other_core, "slab": me},
            device_id_type=MESH,
        )

    def forward_send(chunk, carry):
        def one_pair(p, inner):
            first = pl.multiple_of(chunk * 8 + p * 2, 2)
            both = three_parts(work[pl.ds(first, 2)].reshape(256, 256))
            result = lax.dot_general(
                forward_flip[...], both, (((1,), (1,)), ((), ())), preferred_element_type=F32
            )
            rows = pl.ds(pl.multiple_of(p * 8, 8), 8)
            for part_at in range(2):
                piece = result[128 * part_at : 128 * part_at + 128]
                even, odd = interlaced(
                    piece[:, :128].reshape(16, 8, 128), piece[:, 128:].reshape(16, 8, 128)
                )
                for d in range(16):
                    send_a[chunk, 2 * d, part_at, rows, :] = even[d]
                    send_a[chunk, 2 * d + 1, part_at, rows, :] = odd[d]
            return inner

        lax.fori_loop(0, 4, one_pair, 0)
        for offset in OFFSETS:
            send_copy(send_a, recv_a, send_a_sem, recv_a_sem, chunk, slab_at(offset)).start()
        recv_a[chunk, me] = send_a[chunk, me]
        return carry

    lax.fori_loop(0, 4, forward_send, 0)

    loads[2].wait()

    def flip_spectrum(k, carry):
        piece = spec[pl.ds(k, 128, stride=32), :] * (1.0 / (4096.0 * 4096.0))
        piece = piece.T
        for b in range(4):
            spec_flip[k, pl.ds(b, 32, stride=4), :] = piece[32 * b : 32 * b + 32]
        return carry

    lax.fori_loop(0, 32, flip_spectrum, 0)

    def columns(chunk, carry):
        whole_copy(send_a, recv_a, send_a_sem, recv_a_sem, chunk).wait_recv()

        def down(q, inner):
            rows = pl.ds(pl.multiple_of(q * 8, 8), 8)
            values = [
                (recv_a[chunk, s, 0, rows, :], recv_a[chunk, s, 1, rows, :]) for s in range(32)
            ]
            values = twisted(short_transform(values, -1), -1)
            for k in range(32):
                column[k, rows, 0:128] = values[k][0]
                column[k, rows, 128:256] = values[k][1]
            return inner

        lax.fori_loop(0, 4, down, 0)
        share = pl.ds(pl.multiple_of(chunk * 32, 32), 32)

        def across(g, inner):
            group = pl.ds(pl.multiple_of(g * 8, 8), 8)
            waves = jnp.dot(
                three_parts(column[group].reshape(256, 256)), forward[...],
                preferred_element_type=F32,
            )
            scale = spec_flip[group, share, :].reshape(256, 128)
            waves = jnp.concatenate([waves[:, :128] * scale, waves[:, 128:] * scale], axis=1)
            back = jnp.dot(three_parts(waves), inverse[...], preferred_element_type=F32)
            column[group] = back.reshape(8, 32, 256)
            return inner

        lax.fori_loop(0, 4, across, 0)

        def up(q, inner):
            rows = pl.ds(pl.multiple_of(q * 8, 8), 8)
            values = [(column[k, rows, 0:128], column[k, rows, 128:256]) for k in range(32)]
            values = short_transform(twisted(values, 1), 1)
            for s in range(32):
                send_b[chunk, s, 0, rows, :] = values[s][0]
                send_b[chunk, s, 1, rows, :] = values[s][1]
            return inner

        lax.fori_loop(0, 4, up, 0)
        for offset in OFFSETS:
            send_copy(send_b, recv_b, send_b_sem, recv_b_sem, chunk, slab_at(offset)).start()
        recv_b[chunk, me] = send_b[chunk, me]
        return carry

    lax.fori_loop(0, 4, columns, 0)

    def inverse_rows(chunk, carry):
        whole_copy(send_b, recv_b, send_b_sem, recv_b_sem, chunk).wait_recv()

        def one_pair(p, inner):
            rows = pl.ds(pl.multiple_of(p * 8, 8), 8)
            halves = []
            for part_at in range(2):
                even = jnp.stack([recv_b[chunk, 2 * d, part_at, rows, :] for d in range(16)])
                odd = jnp.stack([recv_b[chunk, 2 * d + 1, part_at, rows, :] for d in range(16)])
                a, b = interlaced(even, odd)
                halves.append((a.reshape(128, 128).T, b.reshape(128, 128).T))
            both = jnp.concatenate(
                [
                    jnp.concatenate([halves[0][i], halves[1][i]], axis=1)
                    for i in range(2)
                ],
                axis=0,
            )
            result = jnp.dot(three_parts(both), inverse[...], preferred_element_type=F32)
            for i in range(2):
                at = chunk * 8 + p * 2 + i
                cos, sin = twist[0, at, 0:1, :], twist[1, at, 0:1, :]
                re = result[128 * i : 128 * i + 128, :128]
                im = result[128 * i : 128 * i + 128, 128:]
                work[at, :, 0:128] = re * cos - im * sin
                work[at, :, 128:256] = re * sin + im * cos
            return inner

        lax.fori_loop(0, 4, one_pair, 0)
        return carry

    lax.fori_loop(0, 4, inverse_rows, 0)

    def member_sum(b):
        for half in range(2):
            rows = pl.ds(pl.multiple_of(b * 16 + half * 8, 8), 8)
            values = [(work[a, rows, 0:128], work[a, rows, 128:256]) for a in range(32)]
            values = short_transform(values, 1)
            for a in range(32):
                field_re[rows, 128 * a : 128 * a + 128] = values[a][0]
                field_im[rows, 128 * a : 128 * a + 128] = values[a][1]
        rows = pl.ds(pl.multiple_of(b * 16, 16), 16)
        part[b] = (
            anom[0, rows, :].astype(F32) * field_re[rows, :]
            + anom[1, rows, :].astype(F32) * field_im[rows, :]
        )

    def to_core(t):
        return pltpu.make_async_remote_copy(
            src_ref=part.at[2 * t + 1 - core],
            dst_ref=recv_part.at[t],
            send_sem=part_sems.at[0, t],
            recv_sem=part_sems.at[1, t],
            device_id={"mem": other_core, "slab": me},
            device_id_type=MESH,
        )

    def to_chip(t):
        return pltpu.make_async_remote_copy(
            src_ref=pair.at[t],
            dst_ref=recv_pair.at[t],
            send_sem=pair_sems.at[0, t],
            recv_sem=pair_sems.at[1, t],
            device_id={"mem": other_chip, "slab": me},
            device_id_type=MESH,
        )

    def finished(t):
        return pltpu.make_async_remote_copy(
            src_ref=total.at[2 * t + core],
            dst_ref=total.at[2 * t + core],
            send_sem=total_sems.at[0, t],
            recv_sem=total_sems.at[1, t],
            device_id={"mem": other_core, "slab": me},
            device_id_type=MESH,
        )

    def write_out(block):
        return pltpu.make_async_copy(
            total.at[block],
            out.at[pl.ds(pl.multiple_of(block * 16, 16), 16), :],
            out_sem.at[block],
        )

    def sum_and_send(t, carry):
        member_sum(2 * t + 1 - core)
        to_core(t).start()
        member_sum(2 * t + core)
        to_core(t).wait_recv()
        pair[t] = part[2 * t + core] + recv_part[t]
        to_chip(t).start()
        return carry

    lax.fori_loop(0, 4, sum_and_send, 0)

    def finish(t, carry):
        to_chip(t).wait_recv()
        total[2 * t + core] = pair[t] + recv_pair[t]
        finished(t).start()
        write_out(2 * t + core).start()
        return carry

    lax.fori_loop(0, 4, finish, 0)

    def collect(t, carry):
        finished(t).wait_recv()
        write_out(2 * t + 1 - core).start()
        return carry

    lax.fori_loop(0, 4, collect, 0)

    def drain(t, carry):
        whole_copy(send_a, recv_a, send_a_sem, recv_a_sem, t).wait_send()
        whole_copy(send_b, recv_b, send_b_sem, recv_b_sem, t).wait_send()
        to_core(t).wait_send()
        to_chip(t).wait_send()
        finished(t).wait_send()
        write_out(2 * t).wait()
        write_out(2 * t + 1).wait()
        return carry

    lax.fori_loop(0, 4, drain, 0)


def per_device(anomalies, increment, spectrum):
    tables, twist = constant_tables()
    vmem = pl.BlockSpec(memory_space=pltpu.VMEM)
    anywhere = pl.BlockSpec(memory_space=pl.ANY)
    dma = pltpu.SemaphoreType.DMA
    return pl.pallas_call(
        kernel,
        out_shape=jax.ShapeDtypeStruct((128, 4096), F32),
        in_specs=[anywhere] * 3 + [vmem] * 4,
        out_specs=anywhere,
        scratch_shapes=[
            pltpu.VMEM((2, 128, 4096), BF16),
            pltpu.VMEM((128, 4096), F32),
            pltpu.VMEM((4096, 128), F32),
            pltpu.VMEM((32, 128, 128), F32),
            pltpu.VMEM((128, 4096), F32),
            pltpu.VMEM((128, 4096), F32),
            pltpu.VMEM((32, 128, 256), F32),
            pltpu.VMEM((4, 32, 2, 32, 128), F32),
            pltpu.VMEM((4, 32, 2, 32, 128), F32),
            pltpu.VMEM((32, 32, 256), F32),
            pltpu.VMEM((4, 32, 2, 32, 128), F32),
            pltpu.VMEM((4, 32, 2, 32, 128), F32),
            pltpu.VMEM((8, 16, 4096), F32),
            pltpu.VMEM((4, 16, 4096), F32),
            pltpu.VMEM((4, 16, 4096), F32),
            pltpu.VMEM((4, 16, 4096), F32),
            pltpu.VMEM((8, 16, 4096), F32),
            dma((3,)),
            dma((4,)), dma((4,)), dma((4,)), dma((4,)),
            dma((2, 4)), dma((2, 4)), dma((2, 4)),
            dma((8,)),
        ],
        compiler_params=pltpu.CompilerParams(
            collective_id=0, has_side_effects=True, vmem_limit_bytes=67043328
        ),
        name="covariance",
    )(anomalies, increment, spectrum, *[jnp.asarray(t) for t in tables], jnp.asarray(twist))


def solution(mesh):
    placed = (P("mem", "slab", None), P("slab", None), P(None, "slab"))
    return jax.shard_map(
        per_device, mesh=mesh, in_specs=placed, out_specs=P("slab", None), check_vma=False
    )
```

profile of v0, /device:TPU:1, one launch (start us, length us, event | category | flops | bytes accessed | tf_op | source)
XLA Modules:
  0.0 138.4 jit_solution(14683458505965331360)
XLA Ops:
  0.0 135.2 %covariance.1 = f32[128,4096]{1,0:T(8,128)} custom-call(bf16[2,128,4096]{2,1,0:T(8,128)(2,1)} %anomalies.1, f32[128,4096]{1,0:T(8,128)} %increment.1, f32[4096,128]{1,0:T(8,128)} %spectrum.1, bf16[256,768]{1,0:T(8,128)(2,1)} %constant.8.clone.forward_flip, bf16[768,256]{1,0:T(8,128)(2,1)} %constant.9.clone.forward, bf16[768,256]{1,0:T(8,128)(2,1)} %constant.10.clone.inverse, ...), custom_call_target="tpu_custom_call" | custom-call | tf_op jit(solution)/shard_map/covariance/pallas_call | solution.py:407
  135.2 3.1 %copy.9 = f32[128,4096]{1,0:T(8,128)} copy(f32[128,4096]{1,0:T(8,128)} %covariance.1) | data formatting | bytes 4194304
where the time goes:
time: 139 us; the launch traced here: 138 us
  Pallas kernels  135 us (97%)
  local copies, waits for them, and re-layouts  3.11 us (2%)
    pallas_call x1, Pallas kernels, per_device(): pl.pallas_call(kernel, out_shape=jax.ShapeDtypeStruct((128, 4096), F32),...  135 us
    unnamed x1, local copies, waits for them, and re-layouts  3.11 us

commit v1 on v0

--- a/solution.py
+++ b/solution.py
@@ -40,7 +40,8 @@
         high = block.astype(BF16)
         low = (block - high.astype(np.float64)).astype(BF16)
         tables.append(np.concatenate([high, high, low], axis=0))
-    twist = 2.0 * np.pi / 4096 * np.outer(np.arange(32), index)
+    order = np.arange(32) % 8 * 4 + np.arange(32) // 8
+    twist = 2.0 * np.pi / 4096 * np.outer(order, index)
     twist = np.stack([np.cos(twist), np.sin(twist)]).astype(np.float32)
     twist = np.broadcast_to(twist[:, :, None, :], (2, 32, 8, 128)).copy()
     return tables, twist
@@ -81,6 +82,10 @@
     return first + second
 
 
+def place_of(wave):
+    return 8 * (wave % 4) + wave // 4
+
+
 def three_parts(x):
     high = x.astype(BF16)
     low = (x - high.astype(F32)).astype(BF16)
@@ -89,10 +94,9 @@
 
 def kernel(
     anomalies, increment, spectrum, forward_flip, forward, inverse, twist, out,
-    anom, incr, spec, spec_flip, field_re, field_im, work, send_a, recv_a,
-    column, send_b, recv_b, part, recv_part, pair, recv_pair, total,
+    anom, wide, incr, spec, turned, spec_flip, work, send_a, recv_a,
+    column, send_b, recv_b, part, recv_part, pair, recv_pair,
     load_sem, send_a_sem, recv_a_sem, send_b_sem, recv_b_sem, part_sems, pair_sems, total_sems,
-    out_sem,
 ):
     me = lax.axis_index("slab")
     mem = lax.axis_index("mem")
@@ -105,13 +109,22 @@
         dz, dy, dx = offset
         return ((z + dz) % 4) * 8 + ((y + dy) % 4) * 2 + (x + dx) % 2
 
-    loads = [
-        pltpu.make_async_copy(anomalies, anom, load_sem.at[0]),
-        pltpu.make_async_copy(increment, incr, load_sem.at[1]),
-        pltpu.make_async_copy(spectrum, spec, load_sem.at[2]),
-    ]
-    for copy in loads:
-        copy.start()
+    def load_anomalies(b):
+        rows = pl.ds(pl.multiple_of(b * 16, 16), 16)
+        return pltpu.make_async_copy(anomalies.at[:, rows, :], anom.at[:, rows, :], load_sem.at[b])
+
+    def load_increment(b):
+        rows = pl.ds(pl.multiple_of(b * 16, 16), 16)
+        return pltpu.make_async_copy(increment.at[rows, :], incr.at[rows, :], load_sem.at[8 + b])
+
+    def start_loads(b, carry):
+        load_anomalies(b).start()
+        load_increment(b).start()
+        return carry
+
+    lax.fori_loop(0, 8, start_loads, 0)
+    load_spectrum = pltpu.make_async_copy(spectrum, spec, load_sem.at[16])
+    load_spectrum.start()
 
     barrier = pltpu.get_barrier_semaphore()
     for offset in OFFSETS:
@@ -135,40 +148,35 @@
         result = [values[0]]
         for k in range(1, 32):
             re, im = values[k]
-            cos, sin = twist[0, k], twist[1, k]
+            cos, sin = twist[0, place_of(k)], twist[1, place_of(k)]
             if sign > 0:
                 result.append((re * cos - im * sin, re * sin + im * cos))
             else:
                 result.append((re * cos + im * sin, im * cos - re * sin))
         return result
 
-    loads[0].wait()
-    loads[1].wait()
-
-    def multiply(b, carry):
+    def first_step(b, carry):
+        load_anomalies(b).wait()
+        load_increment(b).wait()
         rows = pl.ds(pl.multiple_of(b * 16, 16), 16)
-        step = incr[rows, :]
-        field_re[rows, :] = anom[0, rows, :].astype(F32) * step
-        field_im[rows, :] = anom[1, rows, :].astype(F32) * step
-        return carry
-
-    lax.fori_loop(0, 8, multiply, 0)
-
-    def forward_rows(g, carry):
-        rows = pl.ds(pl.multiple_of(g * 8, 8), 8)
-        values = [
-            (field_re[rows, 128 * a : 128 * a + 128], field_im[rows, 128 * a : 128 * a + 128])
-            for a in range(32)
-        ]
-        values = twisted(short_transform(values, -1), -1)
-        for a in range(32):
-            work[a, rows, 0:128] = values[a][0]
-            work[a, rows, 128:256] = values[a][1]
-        return carry
-
-    lax.fori_loop(0, 16, forward_rows, 0)
-
-    pl.semaphore_wait(barrier, len(OFFSETS) + 2)
+        for n in range(8):
+            inputs = []
+            for p in range(4):
+                lanes = slice(128 * (n + 8 * p), 128 * (n + 8 * p) + 128)
+                step = incr[rows, lanes]
+                inputs.append(
+                    (anom[0, rows, lanes].astype(F32) * step, anom[1, rows, lanes].astype(F32) * step)
+                )
+            for c, (re, im) in enumerate(short_transform(inputs, -1)):
+                if c * n:
+                    cos = math.cos(2.0 * math.pi * c * n / 32)
+                    sin = -math.sin(2.0 * math.pi * c * n / 32)
+                    re, im = re * cos - im * sin, re * sin + im * cos
+                work[8 * c + n, rows, 0:128] = re
+                work[8 * c + n, rows, 128:256] = im
+        return carry
+
+    lax.fori_loop(0, 8, first_step, 0)
 
     def send_copy(source, target, send_sem, recv_sem, chunk, slab):
         return pltpu.make_async_remote_copy(
@@ -190,7 +198,21 @@
             device_id_type=MESH,
         )
 
-    def forward_send(chunk, carry):
+    def forward_class(chunk):
+        def second_step(b, inner):
+            rows = pl.ds(pl.multiple_of(b * 16, 16), 16)
+            values = [
+                (work[chunk * 8 + n, rows, 0:128], work[chunk * 8 + n, rows, 128:256])
+                for n in range(8)
+            ]
+            for m, (re, im) in enumerate(short_transform(values, -1)):
+                cos, sin = twist[0, chunk * 8 + m, 0:1, :], twist[1, chunk * 8 + m, 0:1, :]
+                work[chunk * 8 + m, rows, 0:128] = re * cos + im * sin
+                work[chunk * 8 + m, rows, 128:256] = im * cos - re * sin
+            return inner
+
+        lax.fori_loop(0, 8, second_step, 0)
+
         def one_pair(p, inner):
             first = pl.multiple_of(chunk * 8 + p * 2, 2)
             both = three_parts(work[pl.ds(first, 2)].reshape(256, 256))
@@ -209,23 +231,43 @@
             return inner
 
         lax.fori_loop(0, 4, one_pair, 0)
+
+    def forward_send(chunk):
         for offset in OFFSETS:
             send_copy(send_a, recv_a, send_a_sem, recv_a_sem, chunk, slab_at(offset)).start()
         recv_a[chunk, me] = send_a[chunk, me]
-        return carry
-
-    lax.fori_loop(0, 4, forward_send, 0)
-
-    loads[2].wait()
+
+    forward_class(0)
+    pl.semaphore_wait(barrier, len(OFFSETS) + 2)
+    forward_send(0)
+
+    def forward_later(chunk, carry):
+        forward_class(chunk)
+        forward_send(chunk)
+        return carry
+
+    lax.fori_loop(1, 4, forward_later, 0)
+
+    load_spectrum.wait()
 
     def flip_spectrum(k, carry):
         piece = spec[pl.ds(k, 128, stride=32), :] * (1.0 / (4096.0 * 4096.0))
-        piece = piece.T
-        for b in range(4):
-            spec_flip[k, pl.ds(b, 32, stride=4), :] = piece[32 * b : 32 * b + 32]
+        turned[...] = piece.T
+        for c in range(4):
+            for b in range(4):
+                spec_flip[k, pl.ds(32 * c + b, 8, stride=4), :] = turned[
+                    pl.ds(32 * b + c, 8, stride=4), :
+                ]
         return carry
 
     lax.fori_loop(0, 32, flip_spectrum, 0)
+
+    def widen(b, carry):
+        rows = pl.ds(pl.multiple_of(b * 16, 16), 16)
+        wide[:, rows, :] = anom[:, rows, :].astype(F32)
+        return carry
+
+    lax.fori_loop(0, 8, widen, 0)
 
     def columns(chunk, carry):
         whole_copy(send_a, recv_a, send_a_sem, recv_a_sem, chunk).wait_recv()
@@ -309,18 +351,13 @@
     lax.fori_loop(0, 4, inverse_rows, 0)
 
     def member_sum(b):
-        for half in range(2):
-            rows = pl.ds(pl.multiple_of(b * 16 + half * 8, 8), 8)
-            values = [(work[a, rows, 0:128], work[a, rows, 128:256]) for a in range(32)]
-            values = short_transform(values, 1)
-            for a in range(32):
-                field_re[rows, 128 * a : 128 * a + 128] = values[a][0]
-                field_im[rows, 128 * a : 128 * a + 128] = values[a][1]
-        rows = pl.ds(pl.multiple_of(b * 16, 16), 16)
-        part[b] = (
-            anom[0, rows, :].astype(F32) * field_re[rows, :]
-            + anom[1, rows, :].astype(F32) * field_im[rows, :]
-        )
+        rows = pl.ds(pl.multiple_of(b * 8, 8), 8)
+        values = [
+            (work[place_of(a), rows, 0:128], work[place_of(a), rows, 128:256]) for a in range(32)
+        ]
+        for a, (re, im) in enumerate(short_transform(values, 1)):
+            lanes = slice(128 * a, 128 * a + 128)
+            part[b, :, lanes] = wide[0, rows, lanes] * re + wide[1, rows, lanes] * im
 
     def to_core(t):
         return pltpu.make_async_remote_copy(
@@ -342,61 +379,62 @@
             device_id_type=MESH,
         )
 
+    def block_rows(block):
+        return pl.ds(pl.multiple_of(block * 8, 8), 8)
+
     def finished(t):
+        rows = block_rows(2 * t + core)
         return pltpu.make_async_remote_copy(
-            src_ref=total.at[2 * t + core],
-            dst_ref=total.at[2 * t + core],
+            src_ref=out.at[rows, :],
+            dst_ref=out.at[rows, :],
             send_sem=total_sems.at[0, t],
             recv_sem=total_sems.at[1, t],
             device_id={"mem": other_core, "slab": me},
             device_id_type=MESH,
         )
 
-    def write_out(block):
-        return pltpu.make_async_copy(
-            total.at[block],
-            out.at[pl.ds(pl.multiple_of(block * 16, 16), 16), :],
-            out_sem.at[block],
-        )
+    def pass_on(t):
+        to_core(t).wait_recv()
+        pair[t] = part[2 * t + core] + recv_part[t]
+        to_chip(t).start()
 
     def sum_and_send(t, carry):
         member_sum(2 * t + 1 - core)
         to_core(t).start()
         member_sum(2 * t + core)
-        to_core(t).wait_recv()
-        pair[t] = part[2 * t + core] + recv_part[t]
-        to_chip(t).start()
-        return carry
-
-    lax.fori_loop(0, 4, sum_and_send, 0)
+
+        @pl.when(t >= 1)
+        def _():
+            pass_on(t - 1)
+
+        return carry
+
+    lax.fori_loop(0, 8, sum_and_send, 0)
+    pass_on(7)
 
     def finish(t, carry):
         to_chip(t).wait_recv()
-        total[2 * t + core] = pair[t] + recv_pair[t]
+        out[block_rows(2 * t + core), :] = pair[t] + recv_pair[t]
         finished(t).start()
-        write_out(2 * t + core).start()
-        return carry
-
-    lax.fori_loop(0, 4, finish, 0)
-
-    def collect(t, carry):
-        finished(t).wait_recv()
-        write_out(2 * t + 1 - core).start()
-        return carry
-
-    lax.fori_loop(0, 4, collect, 0)
-
-    def drain(t, carry):
+        return carry
+
+    lax.fori_loop(0, 8, finish, 0)
+
+    def drain_slab(t, carry):
         whole_copy(send_a, recv_a, send_a_sem, recv_a_sem, t).wait_send()
         whole_copy(send_b, recv_b, send_b_sem, recv_b_sem, t).wait_send()
+        return carry
+
+    lax.fori_loop(0, 4, drain_slab, 0)
+
+    def drain(t, carry):
         to_core(t).wait_send()
         to_chip(t).wait_send()
         finished(t).wait_send()
-        write_out(2 * t).wait()
-        write_out(2 * t + 1).wait()
-        return carry
-
-    lax.fori_loop(0, 4, drain, 0)
+        finished(t).wait_recv()
+        return carry
+
+    lax.fori_loop(0, 8, drain, 0)
 
 
 def per_device(anomalies, increment, spectrum):
@@ -406,34 +444,32 @@
     dma = pltpu.SemaphoreType.DMA
     return pl.pallas_call(
         kernel,
-        out_shape=jax.ShapeDtypeStruct((128, 4096), F32),
+        out_shape=pltpu.VMEM((128, 4096), F32),
         in_specs=[anywhere] * 3 + [vmem] * 4,
-        out_specs=anywhere,
+        out_specs=vmem,
         scratch_shapes=[
             pltpu.VMEM((2, 128, 4096), BF16),
+            pltpu.VMEM((2, 128, 4096), F32),
             pltpu.VMEM((128, 4096), F32),
             pltpu.VMEM((4096, 128), F32),
+            pltpu.VMEM((128, 128), F32),
             pltpu.VMEM((32, 128, 128), F32),
-            pltpu.VMEM((128, 4096), F32),
-            pltpu.VMEM((128, 4096), F32),
             pltpu.VMEM((32, 128, 256), F32),
             pltpu.VMEM((4, 32, 2, 32, 128), F32),
             pltpu.VMEM((4, 32, 2, 32, 128), F32),
             pltpu.VMEM((32, 32, 256), F32),
             pltpu.VMEM((4, 32, 2, 32, 128), F32),
             pltpu.VMEM((4, 32, 2, 32, 128), F32),
-            pltpu.VMEM((8, 16, 4096), F32),
-            pltpu.VMEM((4, 16, 4096), F32),
-            pltpu.VMEM((4, 16, 4096), F32),
-            pltpu.VMEM((4, 16, 4096), F32),
-            pltpu.VMEM((8, 16, 4096), F32),
-            dma((3,)),
+            pltpu.VMEM((16, 8, 4096), F32),
+            pltpu.VMEM((8, 8, 4096), F32),
+            pltpu.VMEM((8, 8, 4096), F32),
+            pltpu.VMEM((8, 8, 4096), F32),
+            dma((17,)),
             dma((4,)), dma((4,)), dma((4,)), dma((4,)),
-            dma((2, 4)), dma((2, 4)), dma((2, 4)),
-            dma((8,)),
+            dma((2, 8)), dma((2, 8)), dma((2, 8)),
         ],
         compiler_params=pltpu.CompilerParams(
-            collective_id=0, has_side_effects=True, vmem_limit_bytes=67043328
+            collective_id=0, has_side_effects=True, vmem_limit_bytes=58 * 2**20
         ),
         name="covariance",
     )(anomalies, increment, spectrum, *[jnp.asarray(t) for t in tables], jnp.asarray(twist))

time: 139 us -> 135 us (0.971)
  Pallas kernels: 135 us -> 133 us
  local copies, waits for them, and re-layouts: 3.11 us -> 1.32 us
    pallas_call x1, Pallas kernels: 135 us -> 133 us  [per_device(): pl.pallas_call(kernel, out_shape=pltpu.VMEM((128, 4096), F32), in_specs=[...]
    unnamed x1, local copies, waits for them, and re-layouts: 3.11 us -> 1.32 us
where the time goes in v1:
time: 135 us; the launch traced here: 134 us
  Pallas kernels  133 us (99%)
    pallas_call x1, Pallas kernels, per_device(): pl.pallas_call(kernel, out_shape=pltpu.VMEM((128, 4096), F32), in_specs=[...  133 us

profile of v1, /device:TPU:1, one launch (start us, length us, event | category | flops | bytes accessed | tf_op | source)
XLA Modules:
  0.0 134.5 jit_solution(15234049441414672771)
XLA Ops:
  0.0 133.1 %covariance.1 = f32[128,4096]{1,0:T(8,128)S(1)} custom-call(bf16[2,128,4096]{2,1,0:T(8,128)(2,1)} %anomalies.1, f32[128,4096]{1,0:T(8,128)} %increment.1, f32[4096,128]{1,0:T(8,128)} %spectrum.1, bf16[256,768]{1,0:T(8,128)(2,1)} %constant.8.clone.forward_flip, bf16[768,256]{1,0:T(8,128)(2,1)} %constant.9.clone.forward, ...), custom_call_target="tpu_custom_call" | custom-call | tf_op jit(solution)/shard_map/covariance/pallas_call | solution.py:445
  133.2 1.3 copy.9

commit v2 on v1

--- a/solution.py
+++ b/solution.py
@@ -93,7 +93,8 @@
 
 
 def kernel(
-    anomalies, increment, spectrum, forward_flip, forward, inverse, twist, out,
+    anomalies, increment, spectrum, flip_table, forward_table, inverse_table, twist_table, out,
+    forward_flip, forward, inverse, twist,
     anom, wide, incr, spec, turned, spec_flip, work, send_a, recv_a,
     column, send_b, recv_b, part, recv_part, pair, recv_pair,
     load_sem, send_a_sem, recv_a_sem, send_b_sem, recv_b_sem, part_sems, pair_sems, total_sems,
@@ -109,23 +110,6 @@
         dz, dy, dx = offset
         return ((z + dz) % 4) * 8 + ((y + dy) % 4) * 2 + (x + dx) % 2
 
-    def load_anomalies(b):
-        rows = pl.ds(pl.multiple_of(b * 16, 16), 16)
-        return pltpu.make_async_copy(anomalies.at[:, rows, :], anom.at[:, rows, :], load_sem.at[b])
-
-    def load_increment(b):
-        rows = pl.ds(pl.multiple_of(b * 16, 16), 16)
-        return pltpu.make_async_copy(increment.at[rows, :], incr.at[rows, :], load_sem.at[8 + b])
-
-    def start_loads(b, carry):
-        load_anomalies(b).start()
-        load_increment(b).start()
-        return carry
-
-    lax.fori_loop(0, 8, start_loads, 0)
-    load_spectrum = pltpu.make_async_copy(spectrum, spec, load_sem.at[16])
-    load_spectrum.start()
-
     barrier = pltpu.get_barrier_semaphore()
     for offset in OFFSETS:
         pl.semaphore_signal(
@@ -135,6 +119,28 @@
         pl.semaphore_signal(
             barrier, inc=1, device_id={"mem": mate, "slab": me}, device_id_type=MESH
         )
+
+    def load_anomalies(b):
+        rows = pl.ds(pl.multiple_of(b * 16, 16), 16)
+        return pltpu.make_async_copy(anomalies.at[:, rows, :], anom.at[:, rows, :], load_sem.at[b])
+
+    def load_increment(b):
+        rows = pl.ds(pl.multiple_of(b * 16, 16), 16)
+        return pltpu.make_async_copy(increment.at[rows, :], incr.at[rows, :], load_sem.at[8 + b])
+
+    def start_loads(b, carry):
+        load_anomalies(b).start()
+        load_increment(b).start()
+        return carry
+
+    load_twist = pltpu.make_async_copy(twist_table, twist, load_sem.at[17])
+    load_flip = pltpu.make_async_copy(flip_table, forward_flip, load_sem.at[18])
+    load_forward = pltpu.make_async_copy(forward_table, forward, load_sem.at[19])
+    load_inverse = pltpu.make_async_copy(inverse_table, inverse, load_sem.at[20])
+    load_spectrum = pltpu.make_async_copy(spectrum, spec, load_sem.at[16])
+    lax.fori_loop(0, 8, start_loads, 0)
+    for copy in (load_twist, load_flip, load_forward, load_inverse, load_spectrum):
+        copy.start()
 
     sub = lax.broadcasted_iota(jnp.int32, (16, 8, 128), 1)
     lower = sub < 4
@@ -237,6 +243,8 @@
             send_copy(send_a, recv_a, send_a_sem, recv_a_sem, chunk, slab_at(offset)).start()
         recv_a[chunk, me] = send_a[chunk, me]
 
+    load_twist.wait()
+    load_flip.wait()
     forward_class(0)
     pl.semaphore_wait(barrier, len(OFFSETS) + 2)
     forward_send(0)
@@ -248,6 +256,8 @@
 
     lax.fori_loop(1, 4, forward_later, 0)
 
+    load_forward.wait()
+    load_inverse.wait()
     load_spectrum.wait()
 
     def flip_spectrum(k, carry):
@@ -445,9 +455,13 @@
     return pl.pallas_call(
         kernel,
         out_shape=pltpu.VMEM((128, 4096), F32),
-        in_specs=[anywhere] * 3 + [vmem] * 4,
+        in_specs=[anywhere] * 7,
         out_specs=vmem,
         scratch_shapes=[
+            pltpu.VMEM((256, 768), BF16),
+            pltpu.VMEM((768, 256), BF16),
+            pltpu.VMEM((768, 256), BF16),
+            pltpu.VMEM((2, 32, 8, 128), F32),
             pltpu.VMEM((2, 128, 4096), BF16),
             pltpu.VMEM((2, 128, 4096), F32),
             pltpu.VMEM((128, 4096), F32),
@@ -464,7 +478,7 @@
             pltpu.VMEM((8, 8, 4096), F32),
             pltpu.VMEM((8, 8, 4096), F32),
             pltpu.VMEM((8, 8, 4096), F32),
-            dma((17,)),
+            dma((21,)),
             dma((4,)), dma((4,)), dma((4,)), dma((4,)),
             dma((2, 8)), dma((2, 8)), dma((2, 8)),
         ],

time: 135 us -> 134 us (level)
  no operation moved by 1% of the time
where the time goes in v2:
time: 134 us
  Pallas kernels  132 us (99%)
    pallas_call x1, Pallas kernels, per_device(): pl.pallas_call(kernel, out_shape=pltpu.VMEM((128, 4096), F32), in_specs=[...  132 us

profile of v2, /device:TPU:1, one launch (start us, length us, event | category | flops | bytes accessed | tf_op | source)
XLA Modules:
  0.0 133.5 jit_solution(15923543933836042035)
XLA Ops:
  0.0 132.2 %covariance.1 = f32[128,4096]{1,0:T(8,128)S(1)} custom-call(bf16[2,128,4096]{2,1,0:T(8,128)(2,1)} %anomalies.1, f32[128,4096]{1,0:T(8,128)} %increment.1, f32[4096,128]{1,0:T(8,128)} %spectrum.1, bf16[256,768]{1,0:T(8,128)(2,1)} %constant.8.clone.flip_table, bf16[768,256]{1,0:T(8,128)(2,1)} %constant.9.clone.forward_table, ...), custom_call_target="tpu_custom_call" | custom-call | tf_op jit(solution)/shard_map/covariance/pallas_call | solution.py:455
  132.2 1.3 copy.9

commit v3 on v2

--- a/solution.py
+++ b/solution.py
@@ -12,6 +12,9 @@
 F32 = jnp.float32
 BF16 = jnp.bfloat16
 ROOT_HALF = math.sqrt(0.5)
+CLASSES = 8
+SIZE = 32 // CLASSES
+ROWS = 4 * SIZE
 
 ROUNDS = (
     (2, 2), (1, 1), (3, 3), (0, 0), (1, 3), (3, 1), (0, 2), (2, 0),
@@ -40,7 +43,7 @@
         high = block.astype(BF16)
         low = (block - high.astype(np.float64)).astype(BF16)
         tables.append(np.concatenate([high, high, low], axis=0))
-    order = np.arange(32) % 8 * 4 + np.arange(32) // 8
+    order = np.arange(32) % SIZE * CLASSES + np.arange(32) // SIZE
     twist = 2.0 * np.pi / 4096 * np.outer(order, index)
     twist = np.stack([np.cos(twist), np.sin(twist)]).astype(np.float32)
     twist = np.broadcast_to(twist[:, :, None, :], (2, 32, 8, 128)).copy()
@@ -83,7 +86,7 @@
 
 
 def place_of(wave):
-    return 8 * (wave % 4) + wave // 4
+    return SIZE * (wave % CLASSES) + wave // CLASSES
 
 
 def three_parts(x):
@@ -165,10 +168,10 @@
         load_anomalies(b).wait()
         load_increment(b).wait()
         rows = pl.ds(pl.multiple_of(b * 16, 16), 16)
-        for n in range(8):
+        for n in range(SIZE):
             inputs = []
-            for p in range(4):
-                lanes = slice(128 * (n + 8 * p), 128 * (n + 8 * p) + 128)
+            for p in range(CLASSES):
+                lanes = slice(128 * (n + SIZE * p), 128 * (n + SIZE * p) + 128)
                 step = incr[rows, lanes]
                 inputs.append(
                     (anom[0, rows, lanes].astype(F32) * step, anom[1, rows, lanes].astype(F32) * step)
@@ -178,8 +181,8 @@
                     cos = math.cos(2.0 * math.pi * c * n / 32)
                     sin = -math.sin(2.0 * math.pi * c * n / 32)
                     re, im = re * cos - im * sin, re * sin + im * cos
-                work[8 * c + n, rows, 0:128] = re
-                work[8 * c + n, rows, 128:256] = im
+                work[SIZE * c + n, rows, 0:128] = re
+                work[SIZE * c + n, rows, 128:256] = im
         return carry
 
     lax.fori_loop(0, 8, first_step, 0)
@@ -208,19 +211,20 @@
         def second_step(b, inner):
             rows = pl.ds(pl.multiple_of(b * 16, 16), 16)
             values = [
-                (work[chunk * 8 + n, rows, 0:128], work[chunk * 8 + n, rows, 128:256])
-                for n in range(8)
+                (work[chunk * SIZE + n, rows, 0:128], work[chunk * SIZE + n, rows, 128:256])
+                for n in range(SIZE)
             ]
             for m, (re, im) in enumerate(short_transform(values, -1)):
-                cos, sin = twist[0, chunk * 8 + m, 0:1, :], twist[1, chunk * 8 + m, 0:1, :]
-                work[chunk * 8 + m, rows, 0:128] = re * cos + im * sin
-                work[chunk * 8 + m, rows, 128:256] = im * cos - re * sin
+                at = chunk * SIZE + m
+                cos, sin = twist[0, at, 0:1, :], twist[1, at, 0:1, :]
+                work[at, rows, 0:128] = re * cos + im * sin
+                work[at, rows, 128:256] = im * cos - re * sin
             return inner
 
         lax.fori_loop(0, 8, second_step, 0)
 
         def one_pair(p, inner):
-            first = pl.multiple_of(chunk * 8 + p * 2, 2)
+            first = pl.multiple_of(chunk * SIZE + p * 2, 2)
             both = three_parts(work[pl.ds(first, 2)].reshape(256, 256))
             result = lax.dot_general(
                 forward_flip[...], both, (((1,), (1,)), ((), ())), preferred_element_type=F32
@@ -236,7 +240,7 @@
                     send_a[chunk, 2 * d + 1, part_at, rows, :] = odd[d]
             return inner
 
-        lax.fori_loop(0, 4, one_pair, 0)
+        lax.fori_loop(0, SIZE // 2, one_pair, 0)
 
     def forward_send(chunk):
         for offset in OFFSETS:
@@ -254,7 +258,7 @@
         forward_send(chunk)
         return carry
 
-    lax.fori_loop(1, 4, forward_later, 0)
+    lax.fori_loop(1, CLASSES, forward_later, 0)
 
     load_forward.wait()
     load_inverse.wait()
@@ -263,10 +267,10 @@
     def flip_spectrum(k, carry):
         piece = spec[pl.ds(k, 128, stride=32), :] * (1.0 / (4096.0 * 4096.0))
         turned[...] = piece.T
-        for c in range(4):
+        for c in range(CLASSES):
             for b in range(4):
-                spec_flip[k, pl.ds(32 * c + b, 8, stride=4), :] = turned[
-                    pl.ds(32 * b + c, 8, stride=4), :
+                spec_flip[k, pl.ds(ROWS * c + b, SIZE, stride=4), :] = turned[
+                    pl.ds(32 * b + c, SIZE, stride=CLASSES), :
                 ]
         return carry
 
@@ -293,11 +297,11 @@
                 column[k, rows, 128:256] = values[k][1]
             return inner
 
-        lax.fori_loop(0, 4, down, 0)
-        share = pl.ds(pl.multiple_of(chunk * 32, 32), 32)
+        lax.fori_loop(0, ROWS // 8, down, 0)
+        share = pl.ds(pl.multiple_of(chunk * ROWS, ROWS), ROWS)
 
         def across(g, inner):
-            group = pl.ds(pl.multiple_of(g * 8, 8), 8)
+            group = pl.ds(pl.multiple_of(g * 256 // ROWS, 256 // ROWS), 256 // ROWS)
             waves = jnp.dot(
                 three_parts(column[group].reshape(256, 256)), forward[...],
                 preferred_element_type=F32,
@@ -305,10 +309,10 @@
             scale = spec_flip[group, share, :].reshape(256, 128)
             waves = jnp.concatenate([waves[:, :128] * scale, waves[:, 128:] * scale], axis=1)
             back = jnp.dot(three_parts(waves), inverse[...], preferred_element_type=F32)
-            column[group] = back.reshape(8, 32, 256)
+            column[group] = back.reshape(256 // ROWS, ROWS, 256)
             return inner
 
-        lax.fori_loop(0, 4, across, 0)
+        lax.fori_loop(0, ROWS // 8, across, 0)
 
         def up(q, inner):
             rows = pl.ds(pl.multiple_of(q * 8, 8), 8)
@@ -319,13 +323,13 @@
                 send_b[chunk, s, 1, rows, :] = values[s][1]
             return inner
 
-        lax.fori_loop(0, 4, up, 0)
+        lax.fori_loop(0, ROWS // 8, up, 0)
         for offset in OFFSETS:
             send_copy(send_b, recv_b, send_b_sem, recv_b_sem, chunk, slab_at(offset)).start()
         recv_b[chunk, me] = send_b[chunk, me]
         return carry
 
-    lax.fori_loop(0, 4, columns, 0)
+    lax.fori_loop(0, CLASSES, columns, 0)
 
     def inverse_rows(chunk, carry):
         whole_copy(send_b, recv_b, send_b_sem, recv_b_sem, chunk).wait_recv()
@@ -347,7 +351,7 @@
             )
             result = jnp.dot(three_parts(both), inverse[...], preferred_element_type=F32)
             for i in range(2):
-                at = chunk * 8 + p * 2 + i
+                at = chunk * SIZE + p * 2 + i
                 cos, sin = twist[0, at, 0:1, :], twist[1, at, 0:1, :]
                 re = result[128 * i : 128 * i + 128, :128]
                 im = result[128 * i : 128 * i + 128, 128:]
@@ -355,10 +359,10 @@
                 work[at, :, 128:256] = re * sin + im * cos
             return inner
 
-        lax.fori_loop(0, 4, one_pair, 0)
-        return carry
-
-    lax.fori_loop(0, 4, inverse_rows, 0)
+        lax.fori_loop(0, SIZE // 2, one_pair, 0)
+        return carry
+
+    lax.fori_loop(0, CLASSES, inverse_rows, 0)
 
     def member_sum(b):
         rows = pl.ds(pl.multiple_of(b * 8, 8), 8)
@@ -435,7 +439,7 @@
         whole_copy(send_b, recv_b, send_b_sem, recv_b_sem, t).wait_send()
         return carry
 
-    lax.fori_loop(0, 4, drain_slab, 0)
+    lax.fori_loop(0, CLASSES, drain_slab, 0)
 
     def drain(t, carry):
         to_core(t).wait_send()
@@ -469,17 +473,17 @@
             pltpu.VMEM((128, 128), F32),
             pltpu.VMEM((32, 128, 128), F32),
             pltpu.VMEM((32, 128, 256), F32),
-            pltpu.VMEM((4, 32, 2, 32, 128), F32),
-            pltpu.VMEM((4, 32, 2, 32, 128), F32),
-            pltpu.VMEM((32, 32, 256), F32),
-            pltpu.VMEM((4, 32, 2, 32, 128), F32),
-            pltpu.VMEM((4, 32, 2, 32, 128), F32),
+            pltpu.VMEM((CLASSES, 32, 2, ROWS, 128), F32),
+            pltpu.VMEM((CLASSES, 32, 2, ROWS, 128), F32),
+            pltpu.VMEM((32, ROWS, 256), F32),
+            pltpu.VMEM((CLASSES, 32, 2, ROWS, 128), F32),
+            pltpu.VMEM((CLASSES, 32, 2, ROWS, 128), F32),
             pltpu.VMEM((16, 8, 4096), F32),
             pltpu.VMEM((8, 8, 4096), F32),
             pltpu.VMEM((8, 8, 4096), F32),
             pltpu.VMEM((8, 8, 4096), F32),
             dma((21,)),
-            dma((4,)), dma((4,)), dma((4,)), dma((4,)),
+            dma((CLASSES,)), dma((CLASSES,)), dma((CLASSES,)), dma((CLASSES,)),
             dma((2, 8)), dma((2, 8)), dma((2, 8)),
         ],
         compiler_params=pltpu.CompilerParams(

time: 134 us -> 132 us (0.985)
  no operation moved by 1% of the time
where the time goes in v3:
time: 132 us
  Pallas kernels  131 us (99%)
  local copies, waits for them, and re-layouts  1.32 us (1%)
    pallas_call x1, Pallas kernels, per_device(): pl.pallas_call(kernel, out_shape=pltpu.VMEM((128, 4096), F32), in_specs=[...  131 us

profile of v3, /device:TPU:1, one launch (start us, length us, event | category | flops | bytes accessed | tf_op | source)
XLA Modules:
  0.0 132.4 jit_solution(11456301406913676204)
XLA Ops:
  0.0 131.0 %covariance.1 = f32[128,4096]{1,0:T(8,128)S(1)} custom-call(bf16[2,128,4096]{2,1,0:T(8,128)(2,1)} %anomalies.1, f32[128,4096]{1,0:T(8,128)} %increment.1, f32[4096,128]{1,0:T(8,128)} %spectrum.1, bf16[256,768]{1,0:T(8,128)(2,1)} %constant.8.clone.flip_table, bf16[768,256]{1,0:T(8,128)(2,1)} %constant.9.clone.forward_table, ...), custom_call_target="tpu_custom_call" | custom-call | tf_op jit(solution)/shard_map/covariance/pallas_call | solution.py:459
  131.0 1.3 copy.9

commit v4 on v3

--- a/solution.py
+++ b/solution.py
@@ -14,6 +14,7 @@
 ROOT_HALF = math.sqrt(0.5)
 CLASSES = 8
 SIZE = 32 // CLASSES
+DEFERRED = 3
 ROWS = 4 * SIZE
 
 ROUNDS = (
@@ -99,8 +100,8 @@
     anomalies, increment, spectrum, flip_table, forward_table, inverse_table, twist_table, out,
     forward_flip, forward, inverse, twist,
     anom, wide, incr, spec, turned, spec_flip, work, send_a, recv_a,
-    column, send_b, recv_b, part, recv_part, pair, recv_pair,
-    load_sem, send_a_sem, recv_a_sem, send_b_sem, recv_b_sem, part_sems, pair_sems, total_sems,
+    column, staged, send_b, recv_b, part, recv_part, pair, recv_pair,
+    load_sem, send_a_sem, recv_a_sem, send_b_sem, recv_b_sem, half_sems, part_sems, pair_sems, total_sems,
 ):
     me = lax.axis_index("slab")
     mem = lax.axis_index("mem")
@@ -147,6 +148,7 @@
 
     sub = lax.broadcasted_iota(jnp.int32, (16, 8, 128), 1)
     lower = sub < 4
+    left = lax.broadcasted_iota(jnp.int32, (8, 128), 1) < 64
 
     def interlaced(a, b):
         even = jnp.where(lower, a, pltpu.roll(b, 4, 1))
@@ -207,6 +209,26 @@
             device_id_type=MESH,
         )
 
+    def half_copy(chunk, half, slab):
+        return pltpu.make_async_remote_copy(
+            src_ref=send_b.at[chunk, slab, half],
+            dst_ref=recv_b.at[chunk, me, half],
+            send_sem=half_sems.at[0, half, chunk],
+            recv_sem=half_sems.at[1, half, chunk],
+            device_id={"mem": mem, "slab": slab},
+            device_id_type=MESH,
+        )
+
+    def whole_half(chunk, half):
+        return pltpu.make_async_remote_copy(
+            src_ref=send_b.at[chunk, 0:31, half],
+            dst_ref=recv_b.at[chunk, 0:31, half],
+            send_sem=half_sems.at[0, half, chunk],
+            recv_sem=half_sems.at[1, half, chunk],
+            device_id={"mem": other_core, "slab": me},
+            device_id_type=MESH,
+        )
+
     def forward_class(chunk):
         def second_step(b, inner):
             rows = pl.ds(pl.multiple_of(b * 16, 16), 16)
@@ -240,7 +262,7 @@
                     send_a[chunk, 2 * d + 1, part_at, rows, :] = odd[d]
             return inner
 
-        lax.fori_loop(0, SIZE // 2, one_pair, 0)
+        lax.fori_loop(0, SIZE // 2, one_pair, 0, unroll=True)
 
     def forward_send(chunk):
         for offset in OFFSETS:
@@ -319,50 +341,72 @@
             values = [(column[k, rows, 0:128], column[k, rows, 128:256]) for k in range(32)]
             values = short_transform(twisted(values, 1), 1)
             for s in range(32):
-                send_b[chunk, s, 0, rows, :] = values[s][0]
-                send_b[chunk, s, 1, rows, :] = values[s][1]
+                staged[s, 0, rows, :] = values[s][0]
+                staged[s, 1, rows, :] = values[s][1]
             return inner
 
         lax.fori_loop(0, ROWS // 8, up, 0)
+
+        def pack(g, inner):
+            for i in range(4):
+                for part_at in range(2):
+                    a, b = staged[4 * g + i, part_at, 0:8, :], staged[4 * g + i, part_at, 8:16, :]
+                    send_b[chunk, 4 * g + i, 0, part_at] = jnp.where(left, a, pltpu.roll(b, 64, 1))
+                    send_b[chunk, 4 * g + i, 1, part_at] = jnp.where(left, pltpu.roll(a, 64, 1), b)
+            return inner
+
+        lax.fori_loop(0, 8, pack, 0)
+
+        @pl.when(chunk < CLASSES - DEFERRED)
+        def _():
+            for offset in OFFSETS:
+                send_copy(send_b, recv_b, send_b_sem, recv_b_sem, chunk, slab_at(offset)).start()
+
+        @pl.when(chunk >= CLASSES - DEFERRED)
+        def _():
+            for offset in OFFSETS:
+                half_copy(chunk, 0, slab_at(offset)).start()
+
+        recv_b[chunk, me] = send_b[chunk, me]
+        return carry
+
+    lax.fori_loop(0, CLASSES, columns, 0)
+
+    def send_second(chunk, carry):
         for offset in OFFSETS:
-            send_copy(send_b, recv_b, send_b_sem, recv_b_sem, chunk, slab_at(offset)).start()
-        recv_b[chunk, me] = send_b[chunk, me]
-        return carry
-
-    lax.fori_loop(0, CLASSES, columns, 0)
+            half_copy(chunk, 1, slab_at(offset)).start()
+        return carry
+
+    lax.fori_loop(CLASSES - DEFERRED, CLASSES, send_second, 0)
+
+    def inverse_half(chunk, half):
+        halves = []
+        for part_at in range(2):
+            even = jnp.stack([recv_b[chunk, 2 * d, half, part_at] for d in range(16)])
+            odd = jnp.stack([recv_b[chunk, 2 * d + 1, half, part_at] for d in range(16)])
+            a, b = interlaced(even, odd)
+            halves.append((a.reshape(128, 128).T, b.reshape(128, 128).T))
+        both = jnp.concatenate(
+            [jnp.concatenate([halves[0][i], halves[1][i]], axis=1) for i in range(2)], axis=0
+        )
+        result = jnp.dot(three_parts(both), inverse[...], preferred_element_type=F32)
+        rows = pl.ds(64 * half, 64)
+        for i in range(2):
+            for k in range(2):
+                at = chunk * SIZE + 2 * k + i
+                cos, sin = twist[0, at, 0:1, :], twist[1, at, 0:1, :]
+                first = 128 * i + 64 * k
+                re, im = result[first : first + 64, :128], result[first : first + 64, 128:]
+                work[at, rows, 0:128] = re * cos - im * sin
+                work[at, rows, 128:256] = re * sin + im * cos
 
     def inverse_rows(chunk, carry):
         whole_copy(send_b, recv_b, send_b_sem, recv_b_sem, chunk).wait_recv()
-
-        def one_pair(p, inner):
-            rows = pl.ds(pl.multiple_of(p * 8, 8), 8)
-            halves = []
-            for part_at in range(2):
-                even = jnp.stack([recv_b[chunk, 2 * d, part_at, rows, :] for d in range(16)])
-                odd = jnp.stack([recv_b[chunk, 2 * d + 1, part_at, rows, :] for d in range(16)])
-                a, b = interlaced(even, odd)
-                halves.append((a.reshape(128, 128).T, b.reshape(128, 128).T))
-            both = jnp.concatenate(
-                [
-                    jnp.concatenate([halves[0][i], halves[1][i]], axis=1)
-                    for i in range(2)
-                ],
-                axis=0,
-            )
-            result = jnp.dot(three_parts(both), inverse[...], preferred_element_type=F32)
-            for i in range(2):
-                at = chunk * SIZE + p * 2 + i
-                cos, sin = twist[0, at, 0:1, :], twist[1, at, 0:1, :]
-                re = result[128 * i : 128 * i + 128, :128]
-                im = result[128 * i : 128 * i + 128, 128:]
-                work[at, :, 0:128] = re * cos - im * sin
-                work[at, :, 128:256] = re * sin + im * cos
-            return inner
-
-        lax.fori_loop(0, SIZE // 2, one_pair, 0)
-        return carry
-
-    lax.fori_loop(0, CLASSES, inverse_rows, 0)
+        inverse_half(chunk, 0)
+        inverse_half(chunk, 1)
+        return carry
+
+    lax.fori_loop(0, CLASSES - DEFERRED, inverse_rows, 0)
 
     def member_sum(b):
         rows = pl.ds(pl.multiple_of(b * 8, 8), 8)
@@ -417,14 +461,22 @@
         to_core(t).start()
         member_sum(2 * t + core)
 
-        @pl.when(t >= 1)
+        @pl.when(t % 4 >= 1)
         def _():
             pass_on(t - 1)
 
         return carry
 
-    lax.fori_loop(0, 8, sum_and_send, 0)
-    pass_on(7)
+    for half in range(2):
+
+        def last_rows(chunk, carry, half=half):
+            whole_half(chunk, half).wait_recv()
+            inverse_half(chunk, half)
+            return carry
+
+        lax.fori_loop(CLASSES - DEFERRED, CLASSES, last_rows, 0)
+        lax.fori_loop(4 * half, 4 * half + 4, sum_and_send, 0)
+        pass_on(4 * half + 3)
 
     def finish(t, carry):
         to_chip(t).wait_recv()
@@ -436,10 +488,22 @@
 
     def drain_slab(t, carry):
         whole_copy(send_a, recv_a, send_a_sem, recv_a_sem, t).wait_send()
+        return carry
+
+    lax.fori_loop(0, CLASSES, drain_slab, 0)
+
+    def drain_back(t, carry):
         whole_copy(send_b, recv_b, send_b_sem, recv_b_sem, t).wait_send()
         return carry
 
-    lax.fori_loop(0, CLASSES, drain_slab, 0)
+    lax.fori_loop(0, CLASSES - DEFERRED, drain_back, 0)
+
+    def drain_half(t, carry):
+        whole_half(t, 0).wait_send()
+        whole_half(t, 1).wait_send()
+        return carry
+
+    lax.fori_loop(CLASSES - DEFERRED, CLASSES, drain_half, 0)
 
     def drain(t, carry):
         to_core(t).wait_send()
@@ -476,14 +540,16 @@
             pltpu.VMEM((CLASSES, 32, 2, ROWS, 128), F32),
             pltpu.VMEM((CLASSES, 32, 2, ROWS, 128), F32),
             pltpu.VMEM((32, ROWS, 256), F32),
-            pltpu.VMEM((CLASSES, 32, 2, ROWS, 128), F32),
-            pltpu.VMEM((CLASSES, 32, 2, ROWS, 128), F32),
+            pltpu.VMEM((32, 2, ROWS, 128), F32),
+            pltpu.VMEM((CLASSES, 32, 2, 2, 8, 128), F32),
+            pltpu.VMEM((CLASSES, 32, 2, 2, 8, 128), F32),
             pltpu.VMEM((16, 8, 4096), F32),
             pltpu.VMEM((8, 8, 4096), F32),
             pltpu.VMEM((8, 8, 4096), F32),
             pltpu.VMEM((8, 8, 4096), F32),
             dma((21,)),
             dma((CLASSES,)), dma((CLASSES,)), dma((CLASSES,)), dma((CLASSES,)),
+            dma((2, 2, CLASSES)),
             dma((2, 8)), dma((2, 8)), dma((2, 8)),
         ],
         compiler_params=pltpu.CompilerParams(

time: 132 us -> 128 us (0.970)
  Pallas kernels: 131 us -> 126 us
    pallas_call x1, Pallas kernels: 131 us -> 126 us  [per_device(): pl.pallas_call(kernel, out_shape=pltpu.VMEM((128, 4096), F32), in_specs=[...]
where the time goes in v4:
time: 128 us; the launch traced here: 127 us
  Pallas kernels  126 us (98%)
  local copies, waits for them, and re-layouts  1.32 us (1%)
    pallas_call x1, Pallas kernels, per_device(): pl.pallas_call(kernel, out_shape=pltpu.VMEM((128, 4096), F32), in_specs=[...  126 us

profile of v4, /device:TPU:1, one launch (start us, length us, event | category | flops | bytes accessed | tf_op | source)
XLA Modules:
  0.0 127.4 jit_solution(18096152889983012085)
XLA Ops:
  0.0 126.1 %covariance.1 = f32[128,4096]{1,0:T(8,128)S(1)} custom-call(bf16[2,128,4096]{2,1,0:T(8,128)(2,1)} %anomalies.1, f32[128,4096]{1,0:T(8,128)} %increment.1, f32[4096,128]{1,0:T(8,128)} %spectrum.1, bf16[256,768]{1,0:T(8,128)(2,1)} %constant.8.clone.flip_table, bf16[768,256]{1,0:T(8,128)(2,1)} %constant.9.clone.forward_table, ...), custom_call_target="tpu_custom_call" | custom-call | tf_op jit(solution)/shard_map/covariance/pallas_call | solution.py:523
  126.1 1.3 %copy.9 = f32[128,4096]{1,0:T(8,128)} copy(f32[128,4096]{1,0:T(8,128)S(1)} %covariance.1) | data formatting | bytes 4194304

commit v5 on v4

--- a/solution.py
+++ b/solution.py
@@ -14,7 +14,7 @@
 ROOT_HALF = math.sqrt(0.5)
 CLASSES = 8
 SIZE = 32 // CLASSES
-DEFERRED = 3
+DEFERRED = 8
 ROWS = 4 * SIZE
 
 ROUNDS = (
@@ -99,9 +99,9 @@
 def kernel(
     anomalies, increment, spectrum, flip_table, forward_table, inverse_table, twist_table, out,
     forward_flip, forward, inverse, twist,
-    anom, wide, incr, spec, turned, spec_flip, work, send_a, recv_a,
+    anom, held, given, incr, spec, turned, spec_flip, work, send_a, recv_a,
     column, staged, send_b, recv_b, part, recv_part, pair, recv_pair,
-    load_sem, send_a_sem, recv_a_sem, send_b_sem, recv_b_sem, half_sems, part_sems, pair_sems, total_sems,
+    load_sem, swap_sems, sems_a, sems_b, own_sems, part_sems, pair_sems, total_sems,
 ):
     me = lax.axis_index("slab")
     mem = lax.axis_index("mem")
@@ -109,6 +109,7 @@
     core = mem % 2
     other_core = (mem // 2) * 2 + (1 - core)
     other_chip = (1 - mem // 2) * 2 + core
+    moved = (x + core + 1) % 2
 
     def slab_at(offset):
         dz, dy, dx = offset
@@ -116,9 +117,13 @@
 
     barrier = pltpu.get_barrier_semaphore()
     for offset in OFFSETS:
-        pl.semaphore_signal(
-            barrier, inc=1, device_id={"mem": mem, "slab": slab_at(offset)}, device_id_type=MESH
-        )
+        for mate in (mem, other_chip):
+            pl.semaphore_signal(
+                barrier,
+                inc=1,
+                device_id={"mem": mate, "slab": slab_at(offset)},
+                device_id_type=MESH,
+            )
     for mate in (other_core, other_chip):
         pl.semaphore_signal(
             barrier, inc=1, device_id={"mem": mate, "slab": me}, device_id_type=MESH
@@ -166,9 +171,33 @@
                 result.append((re * cos + im * sin, im * cos - re * sin))
         return result
 
-    def first_step(b, carry):
+    def swap(b):
+        rows = pl.ds(pl.multiple_of(b * 16, 16), 16)
+        return pltpu.make_async_remote_copy(
+            src_ref=given.at[:, rows, :],
+            dst_ref=held.at[:, rows, :],
+            send_sem=swap_sems.at[0, b],
+            recv_sem=swap_sems.at[1, b],
+            device_id={"mem": other_chip, "slab": me},
+            device_id_type=MESH,
+        )
+
+    def widen(b, carry):
         load_anomalies(b).wait()
         load_increment(b).wait()
+        rows = pl.ds(pl.multiple_of(b * 16, 16), 16)
+
+        @pl.when((moved == 1) & (b < 4))
+        def _():
+            given[:, pl.ds(pl.multiple_of((b % 4) * 16, 16), 16), :] = anom[:, rows, :].astype(F32)
+
+        @pl.when((moved == 0) | (b >= 4))
+        def _():
+            held[:, rows, :] = anom[:, rows, :].astype(F32)
+
+        return carry
+
+    def first_step(b, carry):
         rows = pl.ds(pl.multiple_of(b * 16, 16), 16)
         for n in range(SIZE):
             inputs = []
@@ -176,7 +205,7 @@
                 lanes = slice(128 * (n + SIZE * p), 128 * (n + SIZE * p) + 128)
                 step = incr[rows, lanes]
                 inputs.append(
-                    (anom[0, rows, lanes].astype(F32) * step, anom[1, rows, lanes].astype(F32) * step)
+                    (held[0, rows, lanes] * step, held[1, rows, lanes] * step)
                 )
             for c, (re, im) in enumerate(short_transform(inputs, -1)):
                 if c * n:
@@ -187,51 +216,79 @@
                 work[SIZE * c + n, rows, 128:256] = im
         return carry
 
-    lax.fori_loop(0, 8, first_step, 0)
-
-    def send_copy(source, target, send_sem, recv_sem, chunk, slab):
+    lax.fori_loop(4, 8, widen, 0)
+    lax.fori_loop(4, 8, first_step, 0)
+    lax.fori_loop(0, 4, widen, 0)
+
+    def mem_at(other):
+        return ((mem // 2 + other) % 2) * 2 + core
+
+    def half_copy(source, target, sems, chunk, half, slab, mate):
         return pltpu.make_async_remote_copy(
-            src_ref=source.at[chunk, slab],
-            dst_ref=target.at[chunk, me],
-            send_sem=send_sem.at[chunk],
-            recv_sem=recv_sem.at[chunk],
-            device_id={"mem": mem, "slab": slab},
+            src_ref=source.at[chunk, slab, half],
+            dst_ref=target.at[chunk, me, half],
+            send_sem=sems.at[0, half, chunk],
+            recv_sem=sems.at[1, half, chunk],
+            device_id={"mem": mate, "slab": slab},
             device_id_type=MESH,
         )
 
-    def whole_copy(source, target, send_sem, recv_sem, chunk):
+    def all_copies(source, target, sems, chunk, half):
         return pltpu.make_async_remote_copy(
-            src_ref=source.at[chunk, 0:31],
-            dst_ref=target.at[chunk, 0:31],
-            send_sem=send_sem.at[chunk],
-            recv_sem=recv_sem.at[chunk],
-            device_id={"mem": other_core, "slab": me},
+            src_ref=source.at[chunk, 0:31, half],
+            dst_ref=target.at[chunk, 0:31, half],
+            send_sem=sems.at[0, half, chunk],
+            recv_sem=sems.at[1, half, chunk],
+            device_id={"mem": other_chip, "slab": me},
             device_id_type=MESH,
         )
 
-    def half_copy(chunk, half, slab):
+    def own_copy(source, target, way, chunk):
         return pltpu.make_async_remote_copy(
-            src_ref=send_b.at[chunk, slab, half],
-            dst_ref=recv_b.at[chunk, me, half],
-            send_sem=half_sems.at[0, half, chunk],
-            recv_sem=half_sems.at[1, half, chunk],
-            device_id={"mem": mem, "slab": slab},
+            src_ref=source.at[chunk, me, 1],
+            dst_ref=target.at[chunk, me, 1],
+            send_sem=own_sems.at[way, 0, chunk],
+            recv_sem=own_sems.at[way, 1, chunk],
+            device_id={"mem": other_chip, "slab": me},
             device_id_type=MESH,
         )
 
-    def whole_half(chunk, half):
-        return pltpu.make_async_remote_copy(
-            src_ref=send_b.at[chunk, 0:31, half],
-            dst_ref=recv_b.at[chunk, 0:31, half],
-            send_sem=half_sems.at[0, half, chunk],
-            recv_sem=half_sems.at[1, half, chunk],
-            device_id={"mem": other_core, "slab": me},
-            device_id_type=MESH,
-        )
-
-    def forward_class(chunk):
+    def keep_own(source, target, way, chunk, half):
+        if half == 0:
+            target[chunk, me, 0] = source[chunk, me, 0]
+            return
+
+        @pl.when(moved == 1)
+        def _():
+            own_copy(source, target, way, chunk).start()
+
+        @pl.when(moved == 0)
+        def _():
+            target[chunk, me, 1] = source[chunk, me, 1]
+
+    def arrived(source, target, sems, way, chunk, half):
+        all_copies(source, target, sems, chunk, half).wait_recv()
+        if half == 1:
+
+            @pl.when(moved == 1)
+            def _():
+                own_copy(source, target, way, chunk).wait_recv()
+
+    def send_forward(chunk, half):
+        for offset in OFFSETS:
+            mate = mem_at(offset[2] + moved * half)
+            half_copy(send_a, recv_a, sems_a, chunk, half, slab_at(offset), mate).start()
+        keep_own(send_a, recv_a, 0, chunk, half)
+
+    def send_back(chunk, half):
+        for offset in OFFSETS:
+            mate = mem_at(offset[2] + ((moved + offset[2]) % 2) * half)
+            half_copy(send_b, recv_b, sems_b, chunk, half, slab_at(offset), mate).start()
+        keep_own(send_b, recv_b, 1, chunk, half)
+
+    def forward_class(chunk, half):
         def second_step(b, inner):
-            rows = pl.ds(pl.multiple_of(b * 16, 16), 16)
+            rows = pl.ds(pl.multiple_of(64 * half + b * 16, 16), 16)
             values = [
                 (work[chunk * SIZE + n, rows, 0:128], work[chunk * SIZE + n, rows, 128:256])
                 for n in range(SIZE)
@@ -243,44 +300,41 @@
                 work[at, rows, 128:256] = im * cos - re * sin
             return inner
 
-        lax.fori_loop(0, 8, second_step, 0)
-
-        def one_pair(p, inner):
-            first = pl.multiple_of(chunk * SIZE + p * 2, 2)
-            both = three_parts(work[pl.ds(first, 2)].reshape(256, 256))
-            result = lax.dot_general(
-                forward_flip[...], both, (((1,), (1,)), ((), ())), preferred_element_type=F32
+        lax.fori_loop(0, 4, second_step, 0)
+        rows = pl.ds(64 * half, 64)
+        both = three_parts(
+            jnp.concatenate([work[chunk * SIZE + m, rows, :] for m in (0, 2, 1, 3)], axis=0)
+        )
+        result = lax.dot_general(
+            forward_flip[...], both, (((1,), (1,)), ((), ())), preferred_element_type=F32
+        )
+        for part_at in range(2):
+            piece = result[128 * part_at : 128 * part_at + 128]
+            even, odd = interlaced(
+                piece[:, :128].reshape(16, 8, 128), piece[:, 128:].reshape(16, 8, 128)
             )
-            rows = pl.ds(pl.multiple_of(p * 8, 8), 8)
-            for part_at in range(2):
-                piece = result[128 * part_at : 128 * part_at + 128]
-                even, odd = interlaced(
-                    piece[:, :128].reshape(16, 8, 128), piece[:, 128:].reshape(16, 8, 128)
-                )
-                for d in range(16):
-                    send_a[chunk, 2 * d, part_at, rows, :] = even[d]
-                    send_a[chunk, 2 * d + 1, part_at, rows, :] = odd[d]
-            return inner
-
-        lax.fori_loop(0, SIZE // 2, one_pair, 0, unroll=True)
-
-    def forward_send(chunk):
-        for offset in OFFSETS:
-            send_copy(send_a, recv_a, send_a_sem, recv_a_sem, chunk, slab_at(offset)).start()
-        recv_a[chunk, me] = send_a[chunk, me]
+            for d in range(16):
+                send_a[chunk, 2 * d, half, part_at] = even[d]
+                send_a[chunk, 2 * d + 1, half, part_at] = odd[d]
 
     load_twist.wait()
     load_flip.wait()
-    forward_class(0)
-    pl.semaphore_wait(barrier, len(OFFSETS) + 2)
-    forward_send(0)
-
-    def forward_later(chunk, carry):
-        forward_class(chunk)
-        forward_send(chunk)
-        return carry
-
-    lax.fori_loop(1, CLASSES, forward_later, 0)
+    forward_class(0, 1)
+    pl.semaphore_wait(barrier, 2 * len(OFFSETS) + 2)
+
+    @pl.when(moved == 1)
+    def _():
+        for b in range(4):
+            swap(b).start()
+
+    send_forward(0, 1)
+
+    def forward_second(chunk, carry):
+        forward_class(chunk, 1)
+        send_forward(chunk, 1)
+        return carry
+
+    lax.fori_loop(1, CLASSES, forward_second, 0)
 
     load_forward.wait()
     load_inverse.wait()
@@ -298,20 +352,41 @@
 
     lax.fori_loop(0, 32, flip_spectrum, 0)
 
-    def widen(b, carry):
-        rows = pl.ds(pl.multiple_of(b * 16, 16), 16)
-        wide[:, rows, :] = anom[:, rows, :].astype(F32)
-        return carry
-
-    lax.fori_loop(0, 8, widen, 0)
+    def late_step(b, carry):
+        @pl.when(moved == 1)
+        def _():
+            swap(b).wait_recv()
+
+        return first_step(b, carry)
+
+    lax.fori_loop(0, 4, late_step, 0)
+
+    def forward_first(chunk, carry):
+        forward_class(chunk, 0)
+        send_forward(chunk, 0)
+        return carry
+
+    lax.fori_loop(0, CLASSES, forward_first, 0)
 
     def columns(chunk, carry):
-        whole_copy(send_a, recv_a, send_a_sem, recv_a_sem, chunk).wait_recv()
+        arrived(send_a, recv_a, sems_a, 0, chunk, 1)
+        arrived(send_a, recv_a, sems_a, 0, chunk, 0)
+
+        def unpack(g, inner):
+            for i in range(4):
+                for part_at in range(2):
+                    a = recv_a[chunk, 4 * g + i, 0, part_at]
+                    b = recv_a[chunk, 4 * g + i, 1, part_at]
+                    staged[4 * g + i, part_at, 0:8, :] = jnp.where(left, a, pltpu.roll(b, 64, 1))
+                    staged[4 * g + i, part_at, 8:16, :] = jnp.where(left, pltpu.roll(a, 64, 1), b)
+            return inner
+
+        lax.fori_loop(0, 8, unpack, 0)
 
         def down(q, inner):
             rows = pl.ds(pl.multiple_of(q * 8, 8), 8)
             values = [
-                (recv_a[chunk, s, 0, rows, :], recv_a[chunk, s, 1, rows, :]) for s in range(32)
+                (staged[s, 0, rows, :], staged[s, 1, rows, :]) for s in range(32)
             ]
             values = twisted(short_transform(values, -1), -1)
             for k in range(32):
@@ -357,24 +432,18 @@
 
         lax.fori_loop(0, 8, pack, 0)
 
+        send_back(chunk, 1)
+
         @pl.when(chunk < CLASSES - DEFERRED)
         def _():
-            for offset in OFFSETS:
-                send_copy(send_b, recv_b, send_b_sem, recv_b_sem, chunk, slab_at(offset)).start()
-
-        @pl.when(chunk >= CLASSES - DEFERRED)
-        def _():
-            for offset in OFFSETS:
-                half_copy(chunk, 0, slab_at(offset)).start()
-
-        recv_b[chunk, me] = send_b[chunk, me]
+            send_back(chunk, 0)
+
         return carry
 
     lax.fori_loop(0, CLASSES, columns, 0)
 
     def send_second(chunk, carry):
-        for offset in OFFSETS:
-            half_copy(chunk, 1, slab_at(offset)).start()
+        send_back(chunk, 0)
         return carry
 
     lax.fori_loop(CLASSES - DEFERRED, CLASSES, send_second, 0)
@@ -400,14 +469,6 @@
                 work[at, rows, 0:128] = re * cos - im * sin
                 work[at, rows, 128:256] = re * sin + im * cos
 
-    def inverse_rows(chunk, carry):
-        whole_copy(send_b, recv_b, send_b_sem, recv_b_sem, chunk).wait_recv()
-        inverse_half(chunk, 0)
-        inverse_half(chunk, 1)
-        return carry
-
-    lax.fori_loop(0, CLASSES - DEFERRED, inverse_rows, 0)
-
     def member_sum(b):
         rows = pl.ds(pl.multiple_of(b * 8, 8), 8)
         values = [
@@ -415,7 +476,7 @@
         ]
         for a, (re, im) in enumerate(short_transform(values, 1)):
             lanes = slice(128 * a, 128 * a + 128)
-            part[b, :, lanes] = wide[0, rows, lanes] * re + wide[1, rows, lanes] * im
+            part[b, :, lanes] = held[0, rows, lanes] * re + held[1, rows, lanes] * im
 
     def to_core(t):
         return pltpu.make_async_remote_copy(
@@ -467,14 +528,14 @@
 
         return carry
 
-    for half in range(2):
+    for half in (1, 0):
 
         def last_rows(chunk, carry, half=half):
-            whole_half(chunk, half).wait_recv()
+            arrived(send_b, recv_b, sems_b, 1, chunk, half)
             inverse_half(chunk, half)
             return carry
 
-        lax.fori_loop(CLASSES - DEFERRED, CLASSES, last_rows, 0)
+        lax.fori_loop(0, CLASSES, last_rows, 0)
         lax.fori_loop(4 * half, 4 * half + 4, sum_and_send, 0)
         pass_on(4 * half + 3)
 
@@ -487,23 +548,23 @@
     lax.fori_loop(0, 8, finish, 0)
 
     def drain_slab(t, carry):
-        whole_copy(send_a, recv_a, send_a_sem, recv_a_sem, t).wait_send()
+        for half in range(2):
+            all_copies(send_a, recv_a, sems_a, t, half).wait_send()
+            all_copies(send_b, recv_b, sems_b, t, half).wait_send()
+
+        @pl.when(moved == 1)
+        def _():
+            own_copy(send_a, recv_a, 0, t).wait_send()
+            own_copy(send_b, recv_b, 1, t).wait_send()
+
         return carry
 
     lax.fori_loop(0, CLASSES, drain_slab, 0)
 
-    def drain_back(t, carry):
-        whole_copy(send_b, recv_b, send_b_sem, recv_b_sem, t).wait_send()
-        return carry
-
-    lax.fori_loop(0, CLASSES - DEFERRED, drain_back, 0)
-
-    def drain_half(t, carry):
-        whole_half(t, 0).wait_send()
-        whole_half(t, 1).wait_send()
-        return carry
-
-    lax.fori_loop(CLASSES - DEFERRED, CLASSES, drain_half, 0)
+    @pl.when(moved == 1)
+    def _():
+        for b in range(4):
+            swap(b).wait_send()
 
     def drain(t, carry):
         to_core(t).wait_send()
@@ -532,13 +593,14 @@
             pltpu.VMEM((2, 32, 8, 128), F32),
             pltpu.VMEM((2, 128, 4096), BF16),
             pltpu.VMEM((2, 128, 4096), F32),
+            pltpu.VMEM((2, 64, 4096), F32),
             pltpu.VMEM((128, 4096), F32),
             pltpu.VMEM((4096, 128), F32),
             pltpu.VMEM((128, 128), F32),
             pltpu.VMEM((32, 128, 128), F32),
             pltpu.VMEM((32, 128, 256), F32),
-            pltpu.VMEM((CLASSES, 32, 2, ROWS, 128), F32),
-            pltpu.VMEM((CLASSES, 32, 2, ROWS, 128), F32),
+            pltpu.VMEM((CLASSES, 32, 2, 2, 8, 128), F32),
+            pltpu.VMEM((CLASSES, 32, 2, 2, 8, 128), F32),
             pltpu.VMEM((32, ROWS, 256), F32),
             pltpu.VMEM((32, 2, ROWS, 128), F32),
             pltpu.VMEM((CLASSES, 32, 2, 2, 8, 128), F32),
@@ -548,8 +610,8 @@
             pltpu.VMEM((8, 8, 4096), F32),
             pltpu.VMEM((8, 8, 4096), F32),
             dma((21,)),
-            dma((CLASSES,)), dma((CLASSES,)), dma((CLASSES,)), dma((CLASSES,)),
-            dma((2, 2, CLASSES)),
+            dma((2, 4)),
+            dma((2, 2, CLASSES)), dma((2, 2, CLASSES)), dma((2, 2, CLASSES)),
             dma((2, 8)), dma((2, 8)), dma((2, 8)),
         ],
         compiler_params=pltpu.CompilerParams(

time: 128 us -> 124 us (0.969)
  Pallas kernels: 126 us -> 123 us
    pallas_call x1, Pallas kernels: 126 us -> 123 us  [per_device(): pl.pallas_call(kernel, out_shape=pltpu.VMEM((128, 4096), F32), in_specs=[...]
where the time goes in v5:
time: 124 us
  Pallas kernels  123 us (99%)
  local copies, waits for them, and re-layouts  1.32 us (1%)
    pallas_call x1, Pallas kernels, per_device(): pl.pallas_call(kernel, out_shape=pltpu.VMEM((128, 4096), F32), in_specs=[...  123 us

profile of v5, /device:TPU:1, one launch (start us, length us, event | category | flops | bytes accessed | tf_op | source)
XLA Modules:
  0.0 124.1 jit_solution(4968758308617975165)
XLA Ops:
  0.0 122.7 %covariance.1 = f32[128,4096]{1,0:T(8,128)S(1)} custom-call(bf16[2,128,4096]{2,1,0:T(8,128)(2,1)} %anomalies.1, f32[128,4096]{1,0:T(8,128)} %increment.1, f32[4096,128]{1,0:T(8,128)} %spectrum.1, bf16[256,768]{1,0:T(8,128)(2,1)} %constant.8.clone.flip_table, bf16[768,256]{1,0:T(8,128)(2,1)} %constant.9.clone.forward_table, ...), custom_call_target="tpu_custom_call" | custom-call | tf_op jit(solution)/shard_map/covariance/pallas_call | solution.py:584
  122.7 1.3 %copy.9 = f32[128,4096]{1,0:T(8,128)} copy(f32[128,4096]{1,0:T(8,128)S(1)} %covariance.1) | data formatting | bytes 4194304

commit v6 on v5

--- a/solution.py
+++ b/solution.py
@@ -545,7 +545,8 @@
         finished(t).start()
         return carry
 
-    lax.fori_loop(0, 8, finish, 0)
+    lax.fori_loop(4, 8, finish, 0)
+    lax.fori_loop(0, 4, finish, 0)
 
     def drain_slab(t, carry):
         for half in range(2):

time: 124 us -> 123 us (level)
  no operation moved by 1% of the time
where the time goes in v6:
time: 123 us
  Pallas kernels  122 us (99%)
  local copies, waits for them, and re-layouts  1.32 us (1%)
    pallas_call x1, Pallas kernels, per_device(): pl.pallas_call(kernel, out_shape=pltpu.VMEM((128, 4096), F32), in_specs=[...  122 us

profile of v6, /device:TPU:1, one launch (start us, length us, event | category | flops | bytes accessed | tf_op | source)
XLA Modules:
  0.0 123.3 jit_solution(14084130610598161570)
XLA Ops:
  0.0 122.0 %covariance.1 = f32[128,4096]{1,0:T(8,128)S(1)} custom-call(bf16[2,128,4096]{2,1,0:T(8,128)(2,1)} %anomalies.1, f32[128,4096]{1,0:T(8,128)} %increment.1, f32[4096,128]{1,0:T(8,128)} %spectrum.1, bf16[256,768]{1,0:T(8,128)(2,1)} %constant.8.clone.flip_table, bf16[768,256]{1,0:T(8,128)(2,1)} %constant.9.clone.forward_table, ...), custom_call_target="tpu_custom_call" | custom-call | tf_op jit(solution)/shard_map/covariance/pallas_call | solution.py:585
  122.0 1.3 %copy.9 = f32[128,4096]{1,0:T(8,128)} copy(f32[128,4096]{1,0:T(8,128)S(1)} %covariance.1) | data formatting | bytes 4194304

commit v7 on v6

--- a/solution.py
+++ b/solution.py
@@ -14,7 +14,8 @@
 ROOT_HALF = math.sqrt(0.5)
 CLASSES = 8
 SIZE = 32 // CLASSES
-DEFERRED = 8
+HELD = 4
+DEFERRED = 7
 ROWS = 4 * SIZE
 
 ROUNDS = (
@@ -331,7 +332,11 @@
 
     def forward_second(chunk, carry):
         forward_class(chunk, 1)
-        send_forward(chunk, 1)
+
+        @pl.when((moved == 0) | (chunk < HELD))
+        def _():
+            send_forward(chunk, 1)
+
         return carry
 
     lax.fori_loop(1, CLASSES, forward_second, 0)
@@ -362,6 +367,10 @@
     lax.fori_loop(0, 4, late_step, 0)
 
     def forward_first(chunk, carry):
+        @pl.when((moved == 1) & (chunk >= HELD))
+        def _():
+            send_forward(chunk, 1)
+
         forward_class(chunk, 0)
         send_forward(chunk, 0)
         return carry

time: 123 us -> 123 us (level)
  no operation moved by 1% of the time
where the time goes in v7:
time: 123 us
  Pallas kernels  122 us (99%)
  local copies, waits for them, and re-layouts  1.32 us (1%)
    pallas_call x1, Pallas kernels, per_device(): pl.pallas_call(kernel, out_shape=pltpu.VMEM((128, 4096), F32), in_specs=[...  122 us

profile of v7, /device:TPU:1, one launch (start us, length us, event | category | flops | bytes accessed | tf_op | source)
XLA Modules:
  0.0 123.1 jit_solution(1696694621302318077)
XLA Ops:
  0.0 121.8 %covariance.1 = f32[128,4096]{1,0:T(8,128)S(1)} custom-call(bf16[2,128,4096]{2,1,0:T(8,128)(2,1)} %anomalies.1, f32[128,4096]{1,0:T(8,128)} %increment.1, f32[4096,128]{1,0:T(8,128)} %spectrum.1, bf16[256,768]{1,0:T(8,128)(2,1)} %constant.8.clone.flip_table, bf16[768,256]{1,0:T(8,128)(2,1)} %constant.9.clone.forward_table, ...), custom_call_target="tpu_custom_call" | custom-call | tf_op jit(solution)/shard_map/covariance/pallas_call | solution.py:594
  121.8 1.3 %copy.9 = f32[128,4096]{1,0:T(8,128)} copy(f32[128,4096]{1,0:T(8,128)S(1)} %covariance.1) | data formatting | bytes 4194304
